TPU v7x, 256 devices: a whole 4x4x8 slice. The times are simulated.
256 devices in a mesh: feat: 64 (over y, z, core), samp: 4 (over x).
Axes of the slice: x: 4, y: 4, z: 8, core: 2. Of those that a mesh axis runs over, the one named last changes fastest.
Arguments:
- design: bfloat16 [14336, 65536], P('samp', 'feat'), may hold values from -0.125 to 0.125
- targets: bfloat16 [14336, 128], P('samp'), may hold values from -26 to 26
- warm_start: float32 [65536, 128], P('feat'), may hold values from -0.6 to 0.6
- active_mask: int32 [2, 65536], P(None, 'feat'), may hold values 0 or 1
- penalty_index: int32 [1], replicated, may hold values from 0 to 7
Outputs:
- coefficients: float32 [65536, 128], P('feat')
- correlations: float32 [3, 65536], P(None, 'feat')
- relative_gaps: float32 [3], replicated
- pruned_counts: float32 [2], replicated
All inputs are finite; a program needn't handle non-finite values. No bound on the sum of `active_mask` on one device may be relied on, other than what follows from the above.
Results may differ from a plain program's by a relative error of at most 0.0024.
The roundings to bfloat16 on the way count: a program that leaves them out, or rounds other values in their place, can miss the bound.
Values may be sent and summed in bfloat16 or wider, within the bound.
No kernel may reach another device: no remote copies, remote signals or barrier semaphores. Data moves between devices by JAX's collectives and lax.ppermute only.
A program may use at most 64 MiB of HBM per device.

v0:
```python
import jax
import jax.numpy as jnp
from jax import lax
from jax.sharding import Mesh
from jax.sharding import PartitionSpec as P

ITERS = 2
FEAT = ("feat_0", "feat_1", "feat_2")
FEAT_SAMP = ("feat_0", "feat_1", "feat_2", "samp")


def copy_for_each(value, axis):
    copies = jnp.broadcast_to(value, (lax.axis_size(axis), *value.shape))
    return lax.all_to_all(copies, axis, split_axis=0, concat_axis=0, tiled=True)


def of_everyone(value, axis):
    return copy_for_each(value, axis).sum(axis=0)


def packed_total(arrays, axis):
    ends = [0]
    for a in arrays:
        ends.append(ends[-1] + a.size)
    running = of_everyone(jnp.concatenate([a.ravel() for a in arrays]), axis)
    return tuple((running[b:e].reshape(a.shape) for a, b, e in zip(arrays, ends, ends[1:])))


def of_everyone_2(value, axis):
    return copy_for_each(value, axis).max(axis=0)


def in_blocks(value, dim, size):
    before, after = (value.shape[:dim], value.shape[dim + 1 :])
    return jnp.moveaxis(value.reshape(*before, size, -1, *after), dim, 0)


def sent_and_summed(value, axis, dim):
    parts = in_blocks(value, dim, lax.axis_size(axis))
    arrived = lax.all_to_all(parts, axis, split_axis=0, concat_axis=0, tiled=True)
    return arrived.sum(axis=0)


def joined_along(parts, dim):
    lengths = list(parts.shape[1:])
    lengths[dim] *= parts.shape[0]
    return jnp.moveaxis(parts, 0, dim).reshape(lengths)


def collect(value, axis, dim):
    return joined_along(copy_for_each(value, axis), dim)


def by_axis(value, axes):
    for axis in axes:
        value = lax.psum(value, axis)
    return value


def group_norms(matrix):
    return jnp.sqrt(jnp.sum(matrix * matrix, axis=1))


def transpose_product(design, right_side):
    return lax.dot_general(
        design, right_side, (((0,), (0,)), ((), ())), preferred_element_type=jnp.float32
    )


def local(design, targets, warm_start, active_mask, penalty_index):
    row_count, col_count = design.shape
    feat_size = lax.axis_size(FEAT)
    feat_slot = lax.axis_index(FEAT)
    block_rows = row_count // feat_size
    samp_first = (lax.axis_index("samp") == 0).astype(jnp.float32)
    corr_local = transpose_product(design, targets)
    squares_local = jnp.sum(jnp.square(design.astype(jnp.float32)), axis=0)
    corr_y, column_squares = packed_total((corr_local, squares_local), "samp")
    penalty_max = of_everyone_2(jnp.max(group_norms(corr_y)), FEAT)
    penalty = penalty_max / (8.0 + 4.0 * penalty_index[0].astype(jnp.float32))
    step_sizes = 0.5 / (1.0 + column_squares)
    current = warm_start
    correlations = []
    relative_gaps = []
    pruned_counts = []
    own_targets = lax.dynamic_slice_in_dim(targets, feat_slot * block_rows, block_rows, 0)
    for iteration in range(ITERS + 1):
        current_half = current.astype(jnp.bfloat16)
        fitted = sent_and_summed(
            jnp.dot(design, current_half, preferred_element_type=jnp.float32), FEAT, 0
        )
        residual = (own_targets.astype(jnp.float32) - fitted).astype(jnp.bfloat16)
        grad_local = transpose_product(design, collect(residual, FEAT, 0))
        resid_float = residual.astype(jnp.float32)
        rr_local = jnp.sum(resid_float * resid_float)
        ry_local = jnp.sum(resid_float * own_targets.astype(jnp.float32))
        bn_local = samp_first * jnp.sum(group_norms(current))
        if iteration < ITERS:
            keep = active_mask[iteration].astype(jnp.float32)
            pruned_local = samp_first * jnp.sum(1.0 - keep)
        else:
            pruned_local = jnp.zeros((), jnp.float32)
        gradient = of_everyone(grad_local, "samp")
        grad_norms = group_norms(gradient)
        local_max = jnp.max(grad_norms)
        grad_top = of_everyone_2(local_max, FEAT)
        rr_sum, ry_sum, bn_sum, pruned_sum = (
            by_axis(rr_local, FEAT_SAMP),
            by_axis(ry_local, FEAT_SAMP),
            by_axis(bn_local, FEAT_SAMP),
            by_axis(pruned_local, FEAT_SAMP),
        )
        scale = jnp.maximum(penalty, grad_top)
        correlations.append(grad_norms / scale)
        primal = 0.5 * rr_sum + penalty * bn_sum
        ratio = penalty / scale
        dual = ratio * ry_sum - 0.5 * ratio * ratio * rr_sum
        relative_gaps.append((primal - dual) / (primal + 1.0))
        if iteration < ITERS:
            pruned_counts.append(pruned_sum)
            moved = current + step_sizes[:, None] * gradient
            moved_norms = group_norms(moved)
            cutoff = step_sizes * penalty
            factor = jnp.maximum(moved_norms - cutoff, 0.0) / jnp.maximum(moved_norms, cutoff)
            current = (keep * factor)[:, None] * moved
    return (current, jnp.stack(correlations), jnp.stack(relative_gaps), jnp.stack(pruned_counts))


def solution(mesh):
    torus = Mesh(
        mesh.devices.reshape(4, 8, 2, mesh.shape["samp"]), ("feat_0", "feat_1", "feat_2", "samp")
    )
    in_specs = (P("samp", FEAT), P("samp", None), P(FEAT, None), P(None, FEAT), P())
    out_specs = (P(FEAT, None), P(None, FEAT), P(), P())
    return jax.shard_map(local, mesh=torus, in_specs=in_specs, out_specs=out_specs, check_vma=False)
```

profile of v0, /device:TPU:1, one launch (start us, length us, event | category | flops | bytes accessed | tf_op | source)
XLA Modules:
  0.0 521.2 jit_solution(8064084640023801377)
XLA Ops:
  0.6 6.5 %fusion.4 = f32[3584,128]{1,0:T(8,128)} fusion(bf16[3584,1024]{1,0:T(8,128)(2,1)} %param.5, f32[1024,128]{1,0:T(8,128)} %param.7), kind=kOutput, calls=%fused_computation.25 | convolution fusion | flops 939655168 | bytes 9699328 | tf_op jit(solution)/shard_map/dot_general | solution.py:90
  7.2 13.1 %all-to-all-start.1 = ((f32[64,56,128]{2,1,0:T(8,128)}), f32[64,56,128]{2,1,0:T(8,128)S(1)}, u32[]{:S(2)}, u32[]{:S(2)}) async-start(f32[64,56,128]{2,1,0:T(8,128)} %bitcast.3), calls=%async_computation.1 | async-start | bytes 3670016 | tf_op jit(solution)/shard_map/all_to_all | solution.py:40
  30.1 35.6 %all-to-all-done.1 = f32[64,56,128]{2,1,0:T(8,128)S(1)} async-done(((f32[64,56,128]{2,1,0:T(8,128)}), f32[64,56,128]{2,1,0:T(8,128)S(1)}, u32[]{:S(2)}, u32[]{:S(2)}) %all-to-all-start.1) | async-done | bytes 1835040 | tf_op jit(solution)/shard_map/all_to_all | solution.py:40
  75.5 23.6 %all-to-all-done = f32[4,1,132096]{2,1,0:T(1,128)S(1)} async-done(((f32[4,1,132096]{2,1,0:T(1,128)}), f32[4,1,132096]{2,1,0:T(1,128)S(1)}, u32[]{:S(2)}, u32[]{:S(2)}) %all-to-all-start) | async-done | bytes 2113568 | tf_op jit(solution)/shard_map/all_to_all | solution.py:14
  100.2 7.1 %all-to-all-start.2 = ((bf16[64,56,128]{2,1,0:T(8,128)(2,1)}), bf16[64,56,128]{2,1,0:T(8,128)(2,1)S(1)}, u32[]{:S(2)}, u32[]{:S(2)}) async-start(bf16[64,56,128]{2,1,0:T(8,128)(2,1)} %broadcast_in_dim.38), calls=%async_computation.2 | async-start | bytes 1835008 | tf_op jit(solution)/shard_map/all_to_all | solution.py:14
  114.3 18.6 %all-to-all-done.2 = bf16[64,56,128]{2,1,0:T(8,128)(2,1)S(1)} async-done(((bf16[64,56,128]{2,1,0:T(8,128)(2,1)}), bf16[64,56,128]{2,1,0:T(8,128)(2,1)S(1)}, u32[]{:S(2)}, u32[]{:S(2)}) %all-to-all-start.2) | async-done | bytes 917536 | tf_op jit(solution)/shard_map/all_to_all | solution.py:14
  134.2 6.2 %all-to-all-start.4 = ((f32[64,1,1]{2,1,0:T(1,128)}), f32[64,1,1]{2,1,0:T(1,128)S(1)}, u32[]{:S(2)}, u32[]{:S(2)}) async-start(f32[64,1,1]{2,1,0:T(1,128)} %broadcast_in_dim.40), calls=%async_computation.4 | async-start | bytes 65536 | tf_op jit(solution)/shard_map/all_to_all | solution.py:14
  157.5 23.0 %all-to-all-done.3 = f32[4,1024,128]{2,1,0:T(8,128)S(1)} async-done(((f32[4,1024,128]{2,1,0:T(8,128)}), f32[4,1024,128]{2,1,0:T(8,128)S(1)}, u32[]{:S(2)}, u32[]{:S(2)}) %all-to-all-start.3) | async-done | bytes 2097184 | tf_op jit(solution)/shard_map/all_to_all | solution.py:14
  182.6 7.1 %convolution_bitcast_fusion.2 = f32[3584,128]{0,1:T(8,128)} fusion(bf16[3584,1024]{1,0:T(8,128)(2,1)} %param.5, f32[1024,128]{1,0:T(8,128)S(1)} %get-tuple-element.61, f32[1024]{0:T(1024)S(1)} %get-tuple-element.67), kind=kOutput, calls=%fused_computation.3 | convolution fusion | flops 939786240 | bytes 9703424 | tf_op jit(solution)/shard_map/dot_general | solution.py:90
  191.6 52.0 %all_to_all.75 = f32[64,56,128]{2,1,0:T(8,128)} all-to-all(f32[64,56,128]{2,1,0:T(8,128)S(1)} %bitcast.48), channel_id=1, replica_groups=mesh['feat_0'=4,'feat_1'=8,'feat_2'=2,'samp'=4] {'feat_0','feat_1','feat..., dimensions={0} | all-to-all | bytes 3670016 | tf_op jit(solution)/shard_map/all_to_all | solution.py:40
  246.0 31.5 %all_to_all.76 = bf16[64,56,128]{2,1,0:T(8,128)(2,1)S(1)} all-to-all(bf16[64,56,128]{2,1,0:T(8,128)(2,1)S(1)} %broadcast_in_dim.41), channel_id=1, replica_groups=mesh['feat_0'=4,'feat_1'=8,'feat_2'=2,'samp'=4] {'feat_0','feat_1','feat..., dimensions={0} | all-to-all | bytes 1835008 | tf_op jit(solution)/shard_map/all_to_all | solution.py:14
  282.2 28.6 %all_to_all.77 = f32[4,1024,128]{2,1,0:T(8,128)S(1)} all-to-all(f32[4,1024,128]{2,1,0:T(8,128)S(1)} %broadcast_in_dim.42), channel_id=1, replica_groups=mesh['feat_0'=4,'feat_1'=8,'feat_2'=2,'samp'=4] {'samp'}, dimensions={0} | all-to-all | bytes 4194304 | tf_op jit(solution)/shard_map/all_to_all | solution.py:14
  321.3 6.8 %all-to-all-start.10 = ((f32[64,56,128]{2,1,0:T(8,128)}), f32[64,56,128]{2,1,0:T(8,128)S(1)}, u32[]{:S(2)}, u32[]{:S(2)}) async-start(f32[64,56,128]{2,1,0:T(8,128)} %bitcast.47), calls=%async_computation.10 | async-start | bytes 3670016 | tf_op jit(solution)/shard_map/all_to_all | solution.py:40
  328.7 44.8 %all-to-all-done.10 = f32[64,56,128]{2,1,0:T(8,128)S(1)} async-done(((f32[64,56,128]{2,1,0:T(8,128)}), f32[64,56,128]{2,1,0:T(8,128)S(1)}, u32[]{:S(2)}, u32[]{:S(2)}) %all-to-all-start.10) | async-done | bytes 1835040 | tf_op jit(solution)/shard_map/all_to_all | solution.py:40
  374.7 6.0 %all-to-all-start.8 = ((f32[64,1,1]{2,1,0:T(1,128)}), f32[64,1,1]{2,1,0:T(1,128)S(1)}, u32[]{:S(2)}, u32[]{:S(2)}) async-start(f32[64,1,1]{2,1,0:T(1,128)} %broadcast_in_dim.43), calls=%async_computation.8 | async-start | bytes 65536 | tf_op jit(solution)/shard_map/all_to_all | solution.py:14
  382.2 7.8 %all-to-all-done.8 = f32[64,1,1]{2,1,0:T(1,128)S(1)} async-done(((f32[64,1,1]{2,1,0:T(1,128)}), f32[64,1,1]{2,1,0:T(1,128)S(1)}, u32[]{:S(2)}, u32[]{:S(2)}) %all-to-all-start.8) | async-done | bytes 288 | tf_op jit(solution)/shard_map/all_to_all | solution.py:14
  396.4 25.1 %all-to-all-done.11 = bf16[64,56,128]{2,1,0:T(8,128)(2,1)S(1)} async-done(((bf16[64,56,128]{2,1,0:T(8,128)(2,1)}), bf16[64,56,128]{2,1,0:T(8,128)(2,1)S(1)}, u32[]{:S(2)}, u32[]{:S(2)}) %all-to-all-start.11) | async-done | bytes 917536 | tf_op jit(solution)/shard_map/all_to_all | solution.py:14
  422.7 6.3 %all-to-all-start.9 = ((f32[64,1,1]{2,1,0:T(1,128)}), f32[64,1,1]{2,1,0:T(1,128)S(1)}, u32[]{:S(2)}, u32[]{:S(2)}) async-start(f32[64,1,1]{2,1,0:T(1,128)} %broadcast_in_dim.44), calls=%async_computation.9 | async-start | bytes 65536 | tf_op jit(solution)/shard_map/all_to_all | solution.py:14
  452.4 7.9 %all-reduce.2 = (f32[]{:T(128)}, f32[]{:T(128)}, f32[]{:T(128)}, f32[]{:T(128)}, f32[]{:T(128)}, /*index=5*/f32[]{:T(128)}, f32[]{:T(128)}, f32[]{:T(128)}, f32[]{:T(128)}, f32[]{:T(128)}, /*index=10*/f32[]{:T(128)}) all-reduce(f32[]{:T(128)} %get-tuple-element.11, ...), channel_id=1, replica_groups=mesh['feat_0'=4,'feat_1'=8,'feat_2'=2,'samp'=4] {'feat_0'}, use_global_device_ids=true, to_apply=%region_55.0 | all-reduce | flops 11 | bytes 88 | tf_op jit(solution)/shard_map/psum | solution.py:56
  460.3 12.6 %all-reduce = (f32[]{:T(128)}, f32[]{:T(128)}, f32[]{:T(128)}, f32[]{:T(128)}, f32[]{:T(128)}, /*index=5*/f32[]{:T(128)}, f32[]{:T(128)}, f32[]{:T(128)}, f32[]{:T(128)}, f32[]{:T(128)}, /*index=10*/f32[]{:T(128)}) all-reduce(f32[]{:T(128)} %get-tuple-element.35, ...), channel_id=1, replica_groups=mesh['feat_0'=4,'feat_1'=8,'feat_2'=2,'samp'=4] {'feat_1'}, use_global_device_ids=true, to_apply=%region_56.0 | all-reduce | flops 11 | bytes 88 | tf_op jit(solution)/shard_map/psum | solution.py:56
  472.9 8.4 %all-reduce.3 = (f32[]{:T(128)}, f32[]{:T(128)}, f32[]{:T(128)}, f32[]{:T(128)}, f32[]{:T(128)}, /*index=5*/f32[]{:T(128)}, f32[]{:T(128)}, f32[]{:T(128)}, f32[]{:T(128)}, f32[]{:T(128)}, /*index=10*/f32[]{:T(128)}) all-reduce(f32[]{:T(128)} %get-tuple-element.13, ...), channel_id=1, replica_groups=mesh['feat_0'=4,'feat_1'=8,'feat_2'=2,'samp'=4] {'feat_2'}, use_global_device_ids=true, to_apply=%region_57.0 | all-reduce | flops 11 | bytes 88 | tf_op jit(solution)/shard_map/psum | solution.py:56
  481.3 9.7 %all-reduce.1 = (f32[]{:T(128)}, f32[]{:T(128)}, f32[]{:T(128)}, f32[]{:T(128)}, f32[]{:T(128)}, /*index=5*/f32[]{:T(128)}, f32[]{:T(128)}, f32[]{:T(128)}, f32[]{:T(128)}, f32[1]{0:T(128)}, /*index=10*/f32[1]{0:T(128)}) all-reduce(f32[]{:T(128)} %get-tuple-element.46, ...), channel_id=1, replica_groups=mesh['feat_0'=4,'feat_1'=8,'feat_2'=2,'samp'=4] {'samp'}, use_global_device_ids=true, to_apply=%region_58.0 | all-reduce | flops 11 | bytes 88 | tf_op jit(solution)/shard_map/psum | solution.py:56
  499.9 7.4 %all-to-all-start.13 = ((f32[64,1,1]{2,1,0:T(1,128)}), f32[64,1,1]{2,1,0:T(1,128)S(1)}, u32[]{:S(2)}, u32[]{:S(2)}) async-start(f32[64,1,1]{2,1,0:T(1,128)} %broadcast_in_dim.47), calls=%async_computation.13 | async-start | bytes 65536 | tf_op jit(solution)/shard_map/all_to_all | solution.py:14
  508.6 7.9 %all-to-all-done.13 = f32[64,1,1]{2,1,0:T(1,128)S(1)} async-done(((f32[64,1,1]{2,1,0:T(1,128)}), f32[64,1,1]{2,1,0:T(1,128)S(1)}, u32[]{:S(2)}, u32[]{:S(2)}) %all-to-all-start.13) | async-done | bytes 288 | tf_op jit(solution)/shard_map/all_to_all | solution.py:14
  (76 shorter events, 100.6 us)
Async XLA Ops:
  0.6 19.7 %copy-start.4 = (bf16[3584,128]{1,0:T(8,128)(2,1)S(1)}, bf16[3584,128]{1,0:T(8,128)(2,1)}, u32[]{:S(2)}) copy-start(bf16[3584,128]{1,0:T(8,128)(2,1)} %param.6) | copy-start | bytes 2752516
  7.2 58.5 %all-to-all-start.1 = ((f32[64,56,128]{2,1,0:T(8,128)}), f32[64,56,128]{2,1,0:T(8,128)S(1)}, u32[]{:S(2)}, u32[]{:S(2)}) async-start(f32[64,56,128]{2,1,0:T(8,128)} %bitcast.3), calls=%async_computation.1 | async-start | bytes 3670016 | tf_op jit(solution)/shard_map/all_to_all | solution.py:40
  65.7 3.5 copy-start
  69.2 30.0 %all-to-all-start = ((f32[4,1,132096]{2,1,0:T(1,128)}), f32[4,1,132096]{2,1,0:T(1,128)S(1)}, u32[]{:S(2)}, u32[]{:S(2)}) async-start(f32[4,1,132096]{2,1,0:T(1,128)} %broadcast_in_dim.37), calls=%async_computation | async-start | bytes 4227072 | tf_op jit(solution)/shard_map/all_to_all | solution.py:14
  100.2 32.8 %all-to-all-start.2 = ((bf16[64,56,128]{2,1,0:T(8,128)(2,1)}), bf16[64,56,128]{2,1,0:T(8,128)(2,1)S(1)}, u32[]{:S(2)}, u32[]{:S(2)}) async-start(bf16[64,56,128]{2,1,0:T(8,128)(2,1)} %broadcast_in_dim.38), calls=%async_computation.2 | async-start | bytes 1835008 | tf_op jit(solution)/shard_map/all_to_all | solution.py:14
  134.2 15.5 %all-to-all-start.4 = ((f32[64,1,1]{2,1,0:T(1,128)}), f32[64,1,1]{2,1,0:T(1,128)S(1)}, u32[]{:S(2)}, u32[]{:S(2)}) async-start(f32[64,1,1]{2,1,0:T(1,128)} %broadcast_in_dim.40), calls=%async_computation.4 | async-start | bytes 65536 | tf_op jit(solution)/shard_map/all_to_all | solution.py:14
  144.7 10.8 %copy-start.3 = (s32[2,1024]{1,0:T(2,128)S(1)}, s32[2,1024]{1,0:T(2,128)}, u32[]{:S(2)}) copy-start(s32[2,1024]{1,0:T(2,128)} %param.8) | copy-start | bytes 24580
  144.7 36.0 %copy-start.1 = (f32[1024,128]{1,0:T(8,128)S(1)}, f32[1024,128]{1,0:T(8,128)}, u32[]{:S(2)}) copy-start(f32[1024,128]{1,0:T(8,128)} %param.7) | copy-start | bytes 1572868
  151.2 29.3 %all-to-all-start.3 = ((f32[4,1024,128]{2,1,0:T(8,128)}), f32[4,1024,128]{2,1,0:T(8,128)S(1)}, u32[]{:S(2)}, u32[]{:S(2)}) async-start(f32[4,1024,128]{2,1,0:T(8,128)} %broadcast_in_dim.39), calls=%async_computation.3 | async-start | bytes 4194304 | tf_op jit(solution)/shard_map/all_to_all | solution.py:14
  313.7 7.6 %copy-start.2 = (f32[1024,128]{1,0:T(8,128)}, f32[1024,128]{1,0:T(8,128)S(1)}, u32[]{:S(2)}) copy-start(f32[1024,128]{1,0:T(8,128)S(1)} %get-tuple-element.58) | copy-start | bytes 1572868
  321.3 52.2 %all-to-all-start.10 = ((f32[64,56,128]{2,1,0:T(8,128)}), f32[64,56,128]{2,1,0:T(8,128)S(1)}, u32[]{:S(2)}, u32[]{:S(2)}) async-start(f32[64,56,128]{2,1,0:T(8,128)} %bitcast.47), calls=%async_computation.10 | async-start | bytes 3670016 | tf_op jit(solution)/shard_map/all_to_all | solution.py:40
  374.7 15.3 %all-to-all-start.8 = ((f32[64,1,1]{2,1,0:T(1,128)}), f32[64,1,1]{2,1,0:T(1,128)S(1)}, u32[]{:S(2)}, u32[]{:S(2)}) async-start(f32[64,1,1]{2,1,0:T(1,128)} %broadcast_in_dim.43), calls=%async_computation.8 | async-start | bytes 65536 | tf_op jit(solution)/shard_map/all_to_all | solution.py:14
  391.0 30.5 %all-to-all-start.11 = ((bf16[64,56,128]{2,1,0:T(8,128)(2,1)}), bf16[64,56,128]{2,1,0:T(8,128)(2,1)S(1)}, u32[]{:S(2)}, u32[]{:S(2)}) async-start(bf16[64,56,128]{2,1,0:T(8,128)(2,1)} %broadcast_in_dim.45), calls=%async_computation.11 | async-start | bytes 1835008 | tf_op jit(solution)/shard_map/all_to_all | solution.py:14
  422.7 15.6 %all-to-all-start.9 = ((f32[64,1,1]{2,1,0:T(1,128)}), f32[64,1,1]{2,1,0:T(1,128)S(1)}, u32[]{:S(2)}, u32[]{:S(2)}) async-start(f32[64,1,1]{2,1,0:T(1,128)} %broadcast_in_dim.44), calls=%async_computation.9 | async-start | bytes 65536 | tf_op jit(solution)/shard_map/all_to_all | solution.py:14
  439.8 57.8 %all-to-all-start.12 = ((f32[4,1024,128]{2,1,0:T(8,128)}), f32[4,1024,128]{2,1,0:T(8,128)S(1)}, u32[]{:S(2)}, u32[]{:S(2)}) async-start(f32[4,1024,128]{2,1,0:T(8,128)} %broadcast_in_dim.46), calls=%async_computation.12 | async-start | bytes 4194304 | tf_op jit(solution)/shard_map/all_to_all | solution.py:14
  499.9 16.7 %all-to-all-start.13 = ((f32[64,1,1]{2,1,0:T(1,128)}), f32[64,1,1]{2,1,0:T(1,128)S(1)}, u32[]{:S(2)}, u32[]{:S(2)}) async-start(f32[64,1,1]{2,1,0:T(1,128)} %broadcast_in_dim.47), calls=%async_computation.13 | async-start | bytes 65536 | tf_op jit(solution)/shard_map/all_to_all | solution.py:14
where the time goes:
time: 523 us; the launch traced here: 521 us
  waiting for transfers between devices  196 us (37%)
  blocking collectives  151 us (29%)
  starting transfers between devices  68.8 us (13%)
  matrix products  37.4 us (7%)
  other arithmetic  33.5 us (6%)
  local copies, waits for them, and re-layouts  17.8 us (3%)
  between operations  16.9 us (3%)
    all_to_all x9, waiting for transfers between devices, copy_for_each(): return lax.all_to_all(copies, axis, split_axis=0, concat_axis=0, tiled=True)  116 us
    all_to_all x2, waiting for transfers between devices, sent_and_summed(): lax.all_to_all(parts, axis, split_axis=0, concat_axis=0, tiled=True)  80.3 us
    all_to_all x2, blocking collectives, copy_for_each(): return lax.all_to_all(copies, axis, split_axis=0, concat_axis=0, tiled=True)  60.1 us
    all_to_all x1, blocking collectives, sent_and_summed(): lax.all_to_all(parts, axis, split_axis=0, concat_axis=0, tiled=True)  52 us
    all_to_all x9, starting transfers between devices, copy_for_each(): return lax.all_to_all(copies, axis, split_axis=0, concat_axis=0, tiled=True)  48.9 us
    psum x4, blocking collectives, by_axis(): value = lax.psum(value, axis)  38.6 us
    all_to_all x2, starting transfers between devices, sent_and_summed(): lax.all_to_all(parts, axis, split_axis=0, concat_axis=0, tiled=True)  19.9 us
    dot_general x3, matrix products, local(): jnp.dot(design, current_half, preferred_element_type=jnp.float32)  19.5 us
  transfers between devices with their start and end apart: 11, of which 10 were waited for; matrix products, arithmetic and copies ran while one was open for 7% of the time, Pallas kernels for 0%

commit v1 on v0

--- a/solution.py
+++ b/solution.py
@@ -53,7 +53,7 @@
 
 def by_axis(value, axes):
     for axis in axes:
-        value = lax.psum(value, axis)
+        value = jnp.sum(lax.all_gather(value, axis), axis=0)
     return value
 
 

time: 523 us -> 658 us (1.26)
  local copies, waits for them, and re-layouts: 17.8 us -> 130 us
  blocking collectives: 151 us -> 199 us
  waiting for transfers between devices: 196 us -> 151 us
  other arithmetic: 33.5 us -> 56.1 us
    unnamed x10 -> x114, local copies, waits for them, and re-layouts: 0.03 us -> 111 us
    all_to_all x1 -> x2, blocking collectives: 52 us -> 102 us  [sent_and_summed(): lax.all_to_all(parts, axis, split_axis=0, concat_axis=0, tiled=True)]
    all_to_all x2 -> x1, waiting for transfers between devices: 80.3 us -> 35.6 us  [sent_and_summed(): lax.all_to_all(parts, axis, split_axis=0, concat_axis=0, tiled=True)]
    psum x4 -> x0, blocking collectives: 38.6 us -> none  [by_axis(): value = lax.psum(value, axis)]
    unnamed x0 -> x4, blocking collectives: none -> 36.1 us
    reduce_sum x0 -> x44, other arithmetic: none -> 26.5 us  [by_axis(): value = jnp.sum(lax.all_gather(value, axis), axis=0)]
    all_to_all x2 -> x1, starting transfers between devices: 19.9 us -> 13.1 us  [sent_and_summed(): lax.all_to_all(parts, axis, split_axis=0, concat_axis=0, tiled=True)]
  transfers between devices with their start and end apart: 11 -> 10, of which waited for: 10 -> 9; matrix products, arithmetic and copies ran while one was open for 7% -> 26% of each run, Pallas kernels for 0% -> 0%
where the time goes in v1:
time: 658 us; the launch traced here: 655 us
  blocking collectives  199 us (30%)
  waiting for transfers between devices  151 us (23%)
  local copies, waits for them, and re-layouts  130 us (20%)
  starting transfers between devices  63.8 us (10%)
  other arithmetic  56.1 us (9%)
  matrix products  38.2 us (6%)
  between operations  17.5 us (3%)
    all_to_all x9, waiting for transfers between devices, copy_for_each(): return lax.all_to_all(copies, axis, split_axis=0, concat_axis=0, tiled=True)  115 us
    unnamed x114, local copies, waits for them, and re-layouts  111 us
    all_to_all x2, blocking collectives, sent_and_summed(): lax.all_to_all(parts, axis, split_axis=0, concat_axis=0, tiled=True)  102 us
    all_to_all x2, blocking collectives, copy_for_each(): return lax.all_to_all(copies, axis, split_axis=0, concat_axis=0, tiled=True)  60.1 us
    all_to_all x9, starting transfers between devices, copy_for_each(): return lax.all_to_all(copies, axis, split_axis=0, concat_axis=0, tiled=True)  50.7 us
    unnamed x4, blocking collectives  36.1 us
    all_to_all x1, waiting for transfers between devices, sent_and_summed(): lax.all_to_all(parts, axis, split_axis=0, concat_axis=0, tiled=True)  35.6 us
    reduce_sum x44, other arithmetic, by_axis(): value = jnp.sum(lax.all_gather(value, axis), axis=0)  26.5 us
  transfers between devices with their start and end apart: 10, of which 9 were waited for; matrix products, arithmetic and copies ran while one was open for 26% of the time, Pallas kernels for 0%

profile of v1, /device:TPU:1, one launch (start us, length us, event | category | flops | bytes accessed | tf_op | source)
XLA Modules:
  0.0 654.9 jit_solution(11867972613454793106)
XLA Ops:
  0.6 6.5 fusion.4
  7.2 13.1 %all-to-all-start.1 = ((f32[64,56,128]{2,1,0:T(8,128)}), f32[64,56,128]{2,1,0:T(8,128)S(1)}, u32[]{:S(2)}, u32[]{:S(2)}) async-start(f32[64,56,128]{2,1,0:T(8,128)} %bitcast.3), calls=%async_computation.1 | async-start | bytes 3670016 | tf_op jit(solution)/shard_map/all_to_all | solution.py:40
  30.1 35.6 %all-to-all-done.1 = f32[64,56,128]{2,1,0:T(8,128)S(1)} async-done(((f32[64,56,128]{2,1,0:T(8,128)}), f32[64,56,128]{2,1,0:T(8,128)S(1)}, u32[]{:S(2)}, u32[]{:S(2)}) %all-to-all-start.1) | async-done | bytes 1835040 | tf_op jit(solution)/shard_map/all_to_all | solution.py:40
  67.5 6.0 all-to-all-start.2
  73.6 25.7 %all-to-all-done.2 = bf16[64,56,128]{2,1,0:T(8,128)(2,1)S(1)} async-done(((bf16[64,56,128]{2,1,0:T(8,128)(2,1)}), bf16[64,56,128]{2,1,0:T(8,128)(2,1)S(1)}, u32[]{:S(2)}, u32[]{:S(2)}) %all-to-all-start.2) | async-done | bytes 917536 | tf_op jit(solution)/shard_map/all_to_all | solution.py:14
  113.0 19.7 %all-to-all-done = f32[4,1,132096]{2,1,0:T(1,128)S(1)} async-done(((f32[4,1,132096]{2,1,0:T(1,128)}), f32[4,1,132096]{2,1,0:T(1,128)S(1)}, u32[]{:S(2)}, u32[]{:S(2)}) %all-to-all-start) | async-done | bytes 2113568 | tf_op jit(solution)/shard_map/all_to_all | solution.py:14
  143.9 19.8 %all-to-all-done.3 = f32[4,1024,128]{2,1,0:T(8,128)} async-done(((f32[4,1024,128]{2,1,0:T(8,128)}), f32[4,1024,128]{2,1,0:T(8,128)}, u32[]{:S(2)}, u32[]{:S(2)}) %all-to-all-start.3) | async-done | bytes 2097184 | tf_op jit(solution)/shard_map/all_to_all | solution.py:14
  165.0 8.4 %all-to-all-start.4 = ((f32[64,1,1]{2,1,0:T(1,128)}), f32[64,1,1]{2,1,0:T(1,128)S(1)}, u32[]{:S(2)}, u32[]{:S(2)}) async-start(f32[64,1,1]{2,1,0:T(1,128)} %broadcast_in_dim.40), calls=%async_computation.4 | async-start | bytes 65536 | tf_op jit(solution)/shard_map/all_to_all | solution.py:14
  176.3 6.2 all-to-all-done.4
  190.5 7.4 %all-to-all-done.8 = f32[64,1,1]{2,1,0:T(1,128)S(1)} async-done(((f32[64,1,1]{2,1,0:T(1,128)}), f32[64,1,1]{2,1,0:T(1,128)S(1)}, u32[]{:S(2)}, u32[]{:S(2)}) %all-to-all-start.8) | async-done | bytes 288 | tf_op jit(solution)/shard_map/all_to_all | solution.py:14
  199.8 7.1 %convolution_bitcast_fusion.2 = f32[3584,128]{0,1:T(8,128)} fusion(bf16[3584,1024]{1,0:T(8,128)(2,1)} %param.5, f32[1024,128]{1,0:T(8,128)S(1)} %get-tuple-element.61, f32[1024]{0:T(1024)S(1)} %get-tuple-element.67), kind=kOutput, calls=%fused_computation.3 | convolution fusion | flops 939786240 | bytes 9703424 | tf_op jit(solution)/shard_map/dot_general | solution.py:90
  208.8 50.1 %all_to_all.76 = f32[64,56,128]{2,1,0:T(8,128)} all-to-all(f32[64,56,128]{2,1,0:T(8,128)S(1)} %bitcast.95), channel_id=1, replica_groups=mesh['feat_0'=4,'feat_1'=8,'feat_2'=2,'samp'=4] {'feat_0','feat_1','feat..., dimensions={0} | all-to-all | bytes 3670016 | tf_op jit(solution)/shard_map/all_to_all | solution.py:40
  261.3 31.5 %all_to_all.75 = bf16[64,56,128]{2,1,0:T(8,128)(2,1)S(1)} all-to-all(bf16[64,56,128]{2,1,0:T(8,128)(2,1)S(1)} %broadcast_in_dim.41), channel_id=1, replica_groups=mesh['feat_0'=4,'feat_1'=8,'feat_2'=2,'samp'=4] {'feat_0','feat_1','feat..., dimensions={0} | all-to-all | bytes 1835008 | tf_op jit(solution)/shard_map/all_to_all | solution.py:14
  297.5 28.6 %all_to_all.77 = f32[4,1024,128]{2,1,0:T(8,128)S(1)} all-to-all(f32[4,1024,128]{2,1,0:T(8,128)S(1)} %broadcast_in_dim.42), channel_id=1, replica_groups=mesh['feat_0'=4,'feat_1'=8,'feat_2'=2,'samp'=4] {'samp'}, dimensions={0} | all-to-all | bytes 4194304 | tf_op jit(solution)/shard_map/all_to_all | solution.py:14
  336.6 52.4 %all_to_all.78 = f32[64,56,128]{2,1,0:T(8,128)S(1)} all-to-all(f32[64,56,128]{2,1,0:T(8,128)} %bitcast.96), channel_id=1, replica_groups=mesh['feat_0'=4,'feat_1'=8,'feat_2'=2,'samp'=4] {'feat_0','feat_1','feat..., dimensions={0} | all-to-all | bytes 3670016 | tf_op jit(solution)/shard_map/all_to_all | solution.py:40
  391.6 6.0 all-to-all-start.11
  398.2 25.1 %all-to-all-done.11 = bf16[64,56,128]{2,1,0:T(8,128)(2,1)S(1)} async-done(((bf16[64,56,128]{2,1,0:T(8,128)(2,1)}), bf16[64,56,128]{2,1,0:T(8,128)(2,1)S(1)}, u32[]{:S(2)}, u32[]{:S(2)}) %all-to-all-start.11) | async-done | bytes 917536 | tf_op jit(solution)/shard_map/all_to_all | solution.py:14
  424.5 6.2 all-to-all-start.9
  466.6 7.2 %all-reduce.46 = (f32[4]{0:T(128)S(1)}, f32[4]{0:T(128)S(1)}, f32[4]{0:T(128)S(1)}, f32[4]{0:T(128)S(1)}, f32[4]{0:T(128)S(1)}, /*index=5*/f32[4]{0:T(128)S(1)},...) all-reduce(f32[4]{0:T(128)S(1)} %dynamic-update-slice.24, ...), channel_id=1, replica_groups=mesh['feat_0'=4,'feat_1'=8,'feat_2'=2,'samp'=4] {'feat_0'}, use_global_device_ids=true, to_apply=%add.24 | all-reduce | flops 44 | bytes 352
  512.8 11.4 %all-reduce.44 = (f32[8]{0:T(128)S(1)}, f32[8]{0:T(128)S(1)}, f32[8]{0:T(128)S(1)}, f32[8]{0:T(128)S(1)}, f32[8]{0:T(128)S(1)}, /*index=5*/f32[8]{0:T(128)S(1)},...) all-reduce(f32[8]{0:T(128)} %dynamic-update-slice.25, ...), channel_id=1, replica_groups=mesh['feat_0'=4,'feat_1'=8,'feat_2'=2,'samp'=4] {'feat_1'}, use_global_device_ids=true, to_apply=%add.25 | all-reduce | flops 88 | bytes 704
  563.0 8.4 %all-reduce.47 = (f32[2]{0:T(128)S(1)}, f32[2]{0:T(128)S(1)}, f32[2]{0:T(128)S(1)}, f32[2]{0:T(128)S(1)}, f32[2]{0:T(128)S(1)}, /*index=5*/f32[2]{0:T(128)S(1)},...) all-reduce(f32[2]{0:T(128)} %dynamic-update-slice.26, ...), channel_id=1, replica_groups=mesh['feat_0'=4,'feat_1'=8,'feat_2'=2,'samp'=4] {'feat_2'}, use_global_device_ids=true, to_apply=%add.26 | all-reduce | flops 22 | bytes 176
  609.9 9.1 %all-reduce.45 = (f32[4]{0:T(128)S(1)}, f32[4]{0:T(128)S(1)}, f32[4]{0:T(128)S(1)}, f32[4]{0:T(128)S(1)}, f32[4]{0:T(128)S(1)}, /*index=5*/f32[4]{0:T(128)S(1)},...) all-reduce(f32[4]{0:T(128)} %dynamic-update-slice.27, ...), channel_id=1, replica_groups=mesh['feat_0'=4,'feat_1'=8,'feat_2'=2,'samp'=4] {'samp'}, use_global_device_ids=true, to_apply=%add.27 | all-reduce | flops 44 | bytes 352
  633.8 7.3 %all-to-all-start.13 = ((f32[64,1,1]{2,1,0:T(1,128)}), f32[64,1,1]{2,1,0:T(1,128)S(1)}, u32[]{:S(2)}, u32[]{:S(2)}) async-start(f32[64,1,1]{2,1,0:T(1,128)} %broadcast_in_dim.47), calls=%async_computation.13 | async-start | bytes 65536 | tf_op jit(solution)/shard_map/all_to_all | solution.py:14
  643.7 6.8 %all-to-all-done.13 = f32[64,1,1]{2,1,0:T(1,128)S(1)} async-done(((f32[64,1,1]{2,1,0:T(1,128)}), f32[64,1,1]{2,1,0:T(1,128)S(1)}, u32[]{:S(2)}, u32[]{:S(2)}) %all-to-all-start.13) | async-done | bytes 288 | tf_op jit(solution)/shard_map/all_to_all | solution.py:14
  (222 shorter events, 231.9 us)
Async XLA Ops:
  0.6 19.7 %copy-start.6 = (bf16[3584,128]{1,0:T(8,128)(2,1)S(1)}, bf16[3584,128]{1,0:T(8,128)(2,1)}, u32[]{:S(2)}) copy-start(bf16[3584,128]{1,0:T(8,128)(2,1)} %param.6) | copy-start | bytes 2752516
  7.2 58.5 %all-to-all-start.1 = ((f32[64,56,128]{2,1,0:T(8,128)}), f32[64,56,128]{2,1,0:T(8,128)S(1)}, u32[]{:S(2)}, u32[]{:S(2)}) async-start(f32[64,56,128]{2,1,0:T(8,128)} %bitcast.3), calls=%async_computation.1 | async-start | bytes 3670016 | tf_op jit(solution)/shard_map/all_to_all | solution.py:40
  65.9 0.6 copy-start.3
  67.5 31.7 %all-to-all-start.2 = ((bf16[64,56,128]{2,1,0:T(8,128)(2,1)}), bf16[64,56,128]{2,1,0:T(8,128)(2,1)S(1)}, u32[]{:S(2)}, u32[]{:S(2)}) async-start(bf16[64,56,128]{2,1,0:T(8,128)(2,1)} %broadcast_in_dim.38), calls=%async_computation.2 | async-start | bytes 1835008 | tf_op jit(solution)/shard_map/all_to_all | solution.py:14
  102.7 30.0 %all-to-all-start = ((f32[4,1,132096]{2,1,0:T(1,128)}), f32[4,1,132096]{2,1,0:T(1,128)S(1)}, u32[]{:S(2)}, u32[]{:S(2)}) async-start(f32[4,1,132096]{2,1,0:T(1,128)} %broadcast_in_dim.37), calls=%async_computation | async-start | bytes 4227072 | tf_op jit(solution)/shard_map/all_to_all | solution.py:14
  111.7 26.9 %copy-start.5 = (s32[2,1024]{1,0:T(2,128)S(1)}, s32[2,1024]{1,0:T(2,128)}, u32[]{:S(2)}) copy-start(s32[2,1024]{1,0:T(2,128)} %param.8) | copy-start | bytes 24580
  111.7 63.4 %copy-start.1 = (f32[1024,128]{1,0:T(8,128)S(1)}, f32[1024,128]{1,0:T(8,128)}, u32[]{:S(2)}) copy-start(f32[1024,128]{1,0:T(8,128)} %param.7) | copy-start | bytes 1572868
  134.2 29.5 %all-to-all-start.3 = ((f32[4,1024,128]{2,1,0:T(8,128)}), f32[4,1024,128]{2,1,0:T(8,128)}, u32[]{:S(2)}, u32[]{:S(2)}) async-start(f32[4,1024,128]{2,1,0:T(8,128)} %broadcast_in_dim.39), calls=%async_computation.3 | async-start | bytes 4194304 | tf_op jit(solution)/shard_map/all_to_all | solution.py:14
  143.1 56.7 %copy-start = (f32[132096]{0:T(1024)}, f32[132096]{0:T(1024)S(1)}, u32[]{:S(2)}) copy-start(f32[132096]{0:T(1024)S(1)} %reduce_sum.649) | copy-start | bytes 1585156
  165.0 17.6 %all-to-all-start.4 = ((f32[64,1,1]{2,1,0:T(1,128)}), f32[64,1,1]{2,1,0:T(1,128)S(1)}, u32[]{:S(2)}, u32[]{:S(2)}) async-start(f32[64,1,1]{2,1,0:T(1,128)} %broadcast_in_dim.40), calls=%async_computation.4 | async-start | bytes 65536 | tf_op jit(solution)/shard_map/all_to_all | solution.py:14
  183.8 14.1 %all-to-all-start.8 = ((f32[64,1,1]{2,1,0:T(1,128)}), f32[64,1,1]{2,1,0:T(1,128)S(1)}, u32[]{:S(2)}, u32[]{:S(2)}) async-start(f32[64,1,1]{2,1,0:T(1,128)} %broadcast_in_dim.43), calls=%async_computation.8 | async-start | bytes 65536 | tf_op jit(solution)/shard_map/all_to_all | solution.py:14
  329.0 60.0 %copy-start.2 = (f32[1024,128]{1,0:T(8,128)}, f32[1024,128]{1,0:T(8,128)S(1)}, u32[]{:S(2)}) copy-start(f32[1024,128]{1,0:T(8,128)S(1)} %get-tuple-element.58) | copy-start | bytes 1572868
  329.0 60.1 %copy-start.4 = (bf16[56,128]{1,0:T(8,128)(2,1)S(1)}, bf16[56,128]{1,0:T(8,128)(2,1)}, u32[]{:S(2)}) copy-start(bf16[56,128]{1,0:T(8,128)(2,1)} %copy-done.3) | copy-start | bytes 43012
  391.6 31.7 %all-to-all-start.11 = ((bf16[64,56,128]{2,1,0:T(8,128)(2,1)}), bf16[64,56,128]{2,1,0:T(8,128)(2,1)S(1)}, u32[]{:S(2)}, u32[]{:S(2)}) async-start(bf16[64,56,128]{2,1,0:T(8,128)(2,1)} %broadcast_in_dim.45), calls=%async_computation.11 | async-start | bytes 1835008 | tf_op jit(solution)/shard_map/all_to_all | solution.py:14
  424.5 15.5 %all-to-all-start.9 = ((f32[64,1,1]{2,1,0:T(1,128)}), f32[64,1,1]{2,1,0:T(1,128)S(1)}, u32[]{:S(2)}, u32[]{:S(2)}) async-start(f32[64,1,1]{2,1,0:T(1,128)} %broadcast_in_dim.44), calls=%async_computation.9 | async-start | bytes 65536 | tf_op jit(solution)/shard_map/all_to_all | solution.py:14
  435.0 10.2 %copy-start.10 = (u32[256]{0:T(256)S(1)}, u32[256]{0:T(256)}, u32[]{:S(2)}) copy-start(u32[256]{0:T(256)} %constant.51) | copy-start | bytes 3076
  435.0 10.8 %copy-start.9 = (u32[256]{0:T(256)S(1)}, u32[256]{0:T(256)}, u32[]{:S(2)}) copy-start(u32[256]{0:T(256)} %constant.56) | copy-start | bytes 3076
  435.0 11.4 %copy-start.8 = (u32[256]{0:T(256)S(1)}, u32[256]{0:T(256)}, u32[]{:S(2)}) copy-start(u32[256]{0:T(256)} %constant.61) | copy-start | bytes 3076
  435.0 12.0 %copy-start.7 = (u32[256]{0:T(256)S(1)}, u32[256]{0:T(256)}, u32[]{:S(2)}) copy-start(u32[256]{0:T(256)} %constant.66) | copy-start | bytes 3076
  441.6 190.0 %all-to-all-start.12 = ((f32[4,1024,128]{2,1,0:T(8,128)}), f32[4,1024,128]{2,1,0:T(8,128)S(1)}, u32[]{:S(2)}, u32[]{:S(2)}) async-start(f32[4,1024,128]{2,1,0:T(8,128)} %broadcast_in_dim.46), calls=%async_computation.12 | async-start | bytes 4194304 | tf_op jit(solution)/shard_map/all_to_all | solution.py:14
  633.8 16.6 %all-to-all-start.13 = ((f32[64,1,1]{2,1,0:T(1,128)}), f32[64,1,1]{2,1,0:T(1,128)S(1)}, u32[]{:S(2)}, u32[]{:S(2)}) async-start(f32[64,1,1]{2,1,0:T(1,128)} %broadcast_in_dim.47), calls=%async_computation.13 | async-start | bytes 65536 | tf_op jit(solution)/shard_map/all_to_all | solution.py:14
